TPU v7x, 32 devices: a whole 2x2x4 slice. The times are simulated.
32 devices in a mesh: gz: 8 (over z, y), xy: 4 (over x, core).
Axes of the slice: x: 2, y: 2, z: 4, core: 2. Of those that a mesh axis runs over, the one named last changes fastest.
Arguments:
- image: float32 [64, 512, 512], P('gz', 'xy'), may hold values from -6 to 6
- offsets: int32 [4, 64, 4, 4], P(None, 'gz', 'xy'), may hold values from -6 to 6
- frac_index: int32 [4, 64, 4, 4], P(None, 'gz', 'xy'), may hold values from 0 to 15
- fractions: float32 [16, 3], replicated, may hold values from 0 to 1
Outputs:
- transported: float32 [64, 512, 512], P('gz', 'xy')
All inputs are finite; a program needn't handle non-finite values.
Results may differ from a plain program's by a relative error of at most 0.0003.
Values sent between devices are 32-bit elements; how exact they have to be, the bound alone decides.
A program may use at most 128 MiB of HBM per device.

v0:
```python
import jax
import jax.numpy as jnp
from jax import lax
from jax.sharding import PartitionSpec as P


def extended(cells, sides, width):
    for axis, dim in sides:
        count = lax.axis_size(axis)
        head = lax.slice_in_dim(cells, 0, width, axis=dim)
        tail = lax.slice_in_dim(cells, cells.shape[dim] - width, cells.shape[dim], axis=dim)
        cells = jnp.concatenate(
            [
                lax.ppermute(tail, axis, [(i, (i + 1) % count) for i in range(count)]),
                cells,
                lax.ppermute(head, axis, [((i + 1) % count, i) for i in range(count)]),
            ],
            axis=dim,
        )
    return cells


def cubic_weights(shares):
    return (
        -shares * (shares - 1.0) * (shares - 2.0) / 6.0,
        (shares + 1.0) * (shares - 1.0) * (shares - 2.0) / 2.0,
        -(shares + 1.0) * shares * (shares - 2.0) / 2.0,
        (shares + 1.0) * shares * (shares - 1.0) / 6.0,
    )


def column_steps(image, offsets, frac_index, fractions):
    step_count = offsets.shape[0]
    all_shifts, all_index = (
        lax.all_gather(offsets, "gz", axis=1, tiled=True),
        lax.all_gather(frac_index, "gz", axis=1, tiled=True),
    )
    standing = jnp.swapaxes(
        lax.all_to_all(image, "gz", split_axis=2, concat_axis=0, tiled=True), 1, 2
    )
    total_planes = standing.shape[0]
    width_y = standing.shape[1]
    width_x = standing.shape[2]
    column_block = lax.axis_index("gz") * width_y // width_x
    block_pick = (jnp.arange(all_shifts.shape[3], dtype=jnp.int32) == column_block).astype(
        jnp.int32
    )
    levels = jnp.arange(total_planes, dtype=jnp.int32)
    table_rows = jnp.arange(fractions.shape[0], dtype=jnp.int32)
    for step_index in range(step_count):
        shifts_now = jnp.sum(all_shifts[step_index, :, 0, :] * block_pick[None, :], axis=1)
        index_now = jnp.sum(all_index[step_index, :, 0, :] * block_pick[None, :], axis=1)
        onehot = (index_now[:, None] == table_rows[None, :]).astype(jnp.float32)
        picked = jnp.dot(onehot, fractions, precision=lax.Precision.HIGHEST)
        zweights = cubic_weights(1.0 - picked[:, 0])
        xweights = cubic_weights(1.0 - picked[:, 1])
        yweights = cubic_weights(1.0 - picked[:, 2])
        rimmed = extended(standing, (("gz", 1), ("xy", 2)), 2)
        merged = jnp.zeros(rimmed.shape, jnp.float32)
        for node in range(4):
            source = jnp.mod(levels - shifts_now - 2 + node, total_planes)
            merged = merged + zweights[node][:, None, None] * jnp.take(rimmed, source, axis=0)
        along_y = jnp.zeros((total_planes, width_y, width_x + 4), jnp.float32)
        for node in range(4):
            along_y = along_y + yweights[node][:, None, None] * merged[:, node : node + width_y, :]
        along_x = jnp.zeros((total_planes, width_y, width_x), jnp.float32)
        for node in range(4):
            along_x = along_x + xweights[node][:, None, None] * along_y[:, :, node : node + width_x]
        standing = along_x
    return lax.all_to_all(
        jnp.swapaxes(standing, 1, 2), "gz", split_axis=0, concat_axis=2, tiled=True
    )


def local(image, offsets, frac_index, fractions):
    return column_steps(image, offsets, frac_index, fractions)


def solution(mesh):
    in_specs = (P("gz", "xy", None), P(None, "gz", "xy", None), P(None, "gz", "xy", None), P())
    out_specs = P("gz", "xy", None)
    return jax.shard_map(local, mesh=mesh, in_specs=in_specs, out_specs=out_specs, check_vma=False)
```

profile of v0, /device:TPU:0, one launch (start us, length us, event | category | flops | bytes accessed | tf_op | source)
XLA Modules:
  0.0 443.2 jit_solution(4297421122283835696)
XLA Ops:
  0.0 2.9 copy.20
  2.9 7.3 %all-to-all-start = ((f32[8,128,512]{1,0,2:T(8,128)}), f32[8,128,512]{1,0,2:T(8,128)S(1)}, u32[]{:S(2)}, u32[]{:S(2)}) async-start(f32[8,128,512]{1,0,2:T(8,128)} %copy.20), calls=%async_computation | async-start | bytes 4194304 | tf_op jit(solution)/shard_map/all_to_all | solution.py:39
  10.5 68.2 %all_gather.6 = s32[4,64,1,4]{3,0,2,1:T(4,128)S(1)} all-gather(s32[4,8,1,4]{3,0,2,1:T(4,128)S(1)} %copy.11), channel_id=1, replica_groups=mesh['gz'=8,'xy'=4] {'gz'}, dimensions={1}, use_global_device_ids=true | all-gather | bytes 4608 | tf_op jit(solution)/shard_map/all_gather | solution.py:36
  78.7 30.5 %all_gather.7 = s32[4,64,1,4]{3,0,2,1:T(4,128)S(1)} all-gather(s32[4,8,1,4]{3,0,2,1:T(4,128)S(1)} %copy.13), channel_id=1, replica_groups=mesh['gz'=8,'xy'=4] {'gz'}, dimensions={1}, use_global_device_ids=true | all-gather | bytes 4608 | tf_op jit(solution)/shard_map/all_gather | solution.py:35
  118.0 8.1 %fusion.160 = (f32[64,2,128]{1,2,0:T(8,128)}, f32[64,2,128]{1,2,0:T(8,128)}) fusion(f32[64,64,128]{1,2,0:T(8,128)} %bitcast.517), kind=kLoop, calls=%fused_computation.473 | loop fusion | bytes 262144 | tf_op jit(solution)/shard_map/slice | solution.py:11
  128.9 2.8 copy.25
  131.8 4.7 %collective-permute-start.1 = (f32[64,2,128]{2,0,1:T(8,128)S(1)}, f32[64,2,128]{2,0,1:T(8,128)S(1)}, u32[]{:S(2)}, u32[]{:S(2)}) collective-permute-start(f32[64,2,128]{2,0,1:T(8,128)S(1)} %copy.25), channel_id=1, source_target_pairs={{4,0},{8,4},{12,8},{16,12},{20,16},{24,20},{28,24},{0,28},{5,1},{9... | collective-permute-start | bytes 196616 | tf_op jit(solution)/shard_map/ppermute | solution.py:16
  147.6 3.9 pad_maximum_fusion
  151.5 5.2 %gather_fusion = f32[64,68,132]{1,2,0:T(8,128)} fusion(f32[64,68,132]{1,2,0:T(8,128)} %pad_maximum_fusion, s32[1024]{0:T(1024)S(1)} %get-tuple-element.145), kind=kCustom, calls=%fused_computation.clone | custom fusion | bytes 4595968 | tf_op jit(solution)/shard_map/jit(_take)/gather | solution.py:62
  156.7 5.1 %gather_fusion.1 = f32[64,68,132]{1,2,0:T(8,128)} fusion(f32[64,68,132]{1,2,0:T(8,128)} %pad_maximum_fusion, s32[1024]{0:T(1024)S(1)} %get-tuple-element.144), kind=kCustom, calls=%fused_computation.1.clone | custom fusion | bytes 4595968 | tf_op jit(solution)/shard_map/jit(_take)/gather | solution.py:62
  161.9 5.2 %gather_fusion.2 = f32[64,68,132]{1,2,0:T(8,128)} fusion(f32[64,68,132]{1,2,0:T(8,128)} %pad_maximum_fusion, s32[1024]{0:T(1024)S(1)} %get-tuple-element.143), kind=kCustom, calls=%fused_computation.2.clone | custom fusion | bytes 4595968 | tf_op jit(solution)/shard_map/jit(_take)/gather | solution.py:62
  167.1 5.2 %gather_fusion.3 = f32[64,68,132]{1,2,0:T(8,128)} fusion(f32[64,68,132]{1,2,0:T(8,128)} %pad_maximum_fusion, s32[1024]{0:T(1024)S(1)} %get-tuple-element.142), kind=kCustom, calls=%fused_computation.3.clone | custom fusion | bytes 4595968 | tf_op jit(solution)/shard_map/jit(_take)/gather | solution.py:62
  172.3 7.3 %fusion.21 = f32[64,68,132]{1,2,0:T(8,128)S(1)} fusion(f32[64,68,132]{1,2,0:T(8,128)} %gather_fusion.3, f32[64,68,132]{1,2,0:T(8,128)} %gather_fusion.2, f32[64,68,132]{1,2,0:T(8,128)} %gather_fusion.1, f32[64,68,132]{1,2,0:T(8,128)} %gather_fusion, f32[64]{0:T(128)S(1)} %get-tuple-element.114, f32[64]{0:T(128)S(1)} %get-tuple-element.115, ...), kind=kLoop, calls=%fused_computation.70 | loop fusion | flops 6319104 | bytes 11490560 | tf_op jit(solution)/shard_map/add | solution.py:62
  179.6 4.5 %fusion.9 = f32[64,64,132]{1,2,0:T(8,128)S(1)} fusion(f32[64,68,132]{1,2,0:T(8,128)S(1)} %fusion.21, f32[64]{0:T(128)S(1)} %get-tuple-element.111, f32[64]{0:T(128)S(1)} %get-tuple-element.112, f32[64]{0:T(128)S(1)} %get-tuple-element.110, f32[64]{0:T(128)S(1)} %get-tuple-element.117), kind=kLoop, calls=%fused_computation.38 | loop fusion | flops 3784704 | bytes 10814464 | tf_op jit(solution)/shard_map/add | solution.py:65
  186.2 4.9 %fusion.159 = (f32[64,2,128]{1,2,0:T(8,128)}, f32[64,2,128]{1,2,0:T(8,128)}) fusion(f32[64,64,128]{1,2,0:T(8,128)S(1)} %fusion.34), kind=kLoop, calls=%fused_computation.472 | loop fusion | bytes 262144 | tf_op jit(solution)/shard_map/slice | solution.py:11
  191.1 2.8 copy.28
  194.0 2.8 copy.29
  196.8 4.7 %collective-permute-start.5 = (f32[64,2,128]{2,0,1:T(8,128)S(1)}, f32[64,2,128]{2,0,1:T(8,128)S(1)}, u32[]{:S(2)}, u32[]{:S(2)}) collective-permute-start(f32[64,2,128]{2,0,1:T(8,128)S(1)} %copy.29), channel_id=1, source_target_pairs={{4,0},{8,4},{12,8},{16,12},{20,16},{24,20},{28,24},{0,28},{5,1},{9... | collective-permute-start | bytes 196616 | tf_op jit(solution)/shard_map/ppermute | solution.py:16
  212.8 3.9 pad_maximum_fusion.1
  216.6 5.2 %gather_fusion.4 = f32[64,68,132]{1,2,0:T(8,128)} fusion(f32[64,68,132]{1,2,0:T(8,128)} %pad_maximum_fusion.1, s32[1024]{0:T(1024)S(1)} %get-tuple-element.149), kind=kCustom, calls=%fused_computation.4.clone | custom fusion | bytes 4595968 | tf_op jit(solution)/shard_map/jit(_take)/gather | solution.py:62
  221.8 5.1 %gather_fusion.5 = f32[64,68,132]{1,2,0:T(8,128)} fusion(f32[64,68,132]{1,2,0:T(8,128)} %pad_maximum_fusion.1, s32[1024]{0:T(1024)S(1)} %get-tuple-element.148), kind=kCustom, calls=%fused_computation.5.clone | custom fusion | bytes 4595968 | tf_op jit(solution)/shard_map/jit(_take)/gather | solution.py:62
  227.0 5.2 %gather_fusion.6 = f32[64,68,132]{1,2,0:T(8,128)} fusion(f32[64,68,132]{1,2,0:T(8,128)} %pad_maximum_fusion.1, s32[1024]{0:T(1024)S(1)} %get-tuple-element.147), kind=kCustom, calls=%fused_computation.6.clone | custom fusion | bytes 4595968 | tf_op jit(solution)/shard_map/jit(_take)/gather | solution.py:62
  232.2 5.2 %gather_fusion.7 = f32[64,68,132]{1,2,0:T(8,128)} fusion(f32[64,68,132]{1,2,0:T(8,128)} %pad_maximum_fusion.1, s32[1024]{0:T(1024)S(1)} %get-tuple-element.146), kind=kCustom, calls=%fused_computation.7.clone | custom fusion | bytes 4595968 | tf_op jit(solution)/shard_map/jit(_take)/gather | solution.py:62
  237.4 7.3 %fusion.18 = f32[64,68,132]{1,2,0:T(8,128)S(1)} fusion(f32[64,68,132]{1,2,0:T(8,128)} %gather_fusion.7, f32[64,68,132]{1,2,0:T(8,128)} %gather_fusion.6, f32[64,68,132]{1,2,0:T(8,128)} %gather_fusion.5, f32[64,68,132]{1,2,0:T(8,128)} %gather_fusion.4, f32[64]{0:T(128)S(1)} %get-tuple-element.102, f32[64]{0:T(128)S(1)} %get-tuple-element.103, ...), kind=kLoop, calls=%fused_computation.63 | loop fusion | flops 6319104 | bytes 11490560 | tf_op jit(solution)/shard_map/add | solution.py:62
  244.7 4.5 %fusion.6 = f32[64,64,132]{1,2,0:T(8,128)S(1)} fusion(f32[64,68,132]{1,2,0:T(8,128)S(1)} %fusion.18, f32[64]{0:T(128)S(1)} %get-tuple-element.99, f32[64]{0:T(128)S(1)} %get-tuple-element.100, f32[64]{0:T(128)S(1)} %get-tuple-element.98, f32[64]{0:T(128)S(1)} %get-tuple-element.105), kind=kLoop, calls=%fused_computation.31 | loop fusion | flops 3784704 | bytes 10814464 | tf_op jit(solution)/shard_map/add | solution.py:65
  251.3 4.9 %fusion.158 = (f32[64,2,128]{1,2,0:T(8,128)}, f32[64,2,128]{1,2,0:T(8,128)}) fusion(f32[64,64,128]{1,2,0:T(8,128)S(1)} %fusion.31), kind=kLoop, calls=%fused_computation.471 | loop fusion | bytes 262144 | tf_op jit(solution)/shard_map/slice | solution.py:11
  259.1 2.8 copy.33
  261.9 4.7 %collective-permute-start.9 = (f32[64,2,128]{2,0,1:T(8,128)S(1)}, f32[64,2,128]{2,0,1:T(8,128)S(1)}, u32[]{:S(2)}, u32[]{:S(2)}) collective-permute-start(f32[64,2,128]{2,0,1:T(8,128)S(1)} %copy.33), channel_id=1, source_target_pairs={{4,0},{8,4},{12,8},{16,12},{20,16},{24,20},{28,24},{0,28},{5,1},{9... | collective-permute-start | bytes 196616 | tf_op jit(solution)/shard_map/ppermute | solution.py:16
  278.1 3.9 pad_maximum_fusion.2
  281.9 5.2 %gather_fusion.8 = f32[64,68,132]{1,2,0:T(8,128)} fusion(f32[64,68,132]{1,2,0:T(8,128)} %pad_maximum_fusion.2, s32[1024]{0:T(1024)S(1)} %get-tuple-element.153), kind=kCustom, calls=%fused_computation.8.clone | custom fusion | bytes 4595968 | tf_op jit(solution)/shard_map/jit(_take)/gather | solution.py:62
  287.1 5.1 %gather_fusion.9 = f32[64,68,132]{1,2,0:T(8,128)} fusion(f32[64,68,132]{1,2,0:T(8,128)} %pad_maximum_fusion.2, s32[1024]{0:T(1024)S(1)} %get-tuple-element.152), kind=kCustom, calls=%fused_computation.9.clone | custom fusion | bytes 4595968 | tf_op jit(solution)/shard_map/jit(_take)/gather | solution.py:62
  292.3 5.2 %gather_fusion.10 = f32[64,68,132]{1,2,0:T(8,128)} fusion(f32[64,68,132]{1,2,0:T(8,128)} %pad_maximum_fusion.2, s32[1024]{0:T(1024)S(1)} %get-tuple-element.151), kind=kCustom, calls=%fused_computation.10.clone | custom fusion | bytes 4595968 | tf_op jit(solution)/shard_map/jit(_take)/gather | solution.py:62
  297.5 5.2 %gather_fusion.11 = f32[64,68,132]{1,2,0:T(8,128)} fusion(f32[64,68,132]{1,2,0:T(8,128)} %pad_maximum_fusion.2, s32[1024]{0:T(1024)S(1)} %get-tuple-element.150), kind=kCustom, calls=%fused_computation.11.clone | custom fusion | bytes 4595968 | tf_op jit(solution)/shard_map/jit(_take)/gather | solution.py:62
  302.7 7.3 %fusion.15 = f32[64,68,132]{1,2,0:T(8,128)S(1)} fusion(f32[64,68,132]{1,2,0:T(8,128)} %gather_fusion.11, f32[64,68,132]{1,2,0:T(8,128)} %gather_fusion.10, f32[64,68,132]{1,2,0:T(8,128)} %gather_fusion.9, f32[64,68,132]{1,2,0:T(8,128)} %gather_fusion.8, f32[64]{0:T(128)S(1)} %get-tuple-element.90, f32[64]{0:T(128)S(1)} %get-tuple-element.91, ...), kind=kLoop, calls=%fused_computation.56 | loop fusion | flops 6319104 | bytes 11490560 | tf_op jit(solution)/shard_map/add | solution.py:62
  310.0 4.5 %fusion.3 = f32[64,64,132]{1,2,0:T(8,128)S(1)} fusion(f32[64,68,132]{1,2,0:T(8,128)S(1)} %fusion.15, f32[64]{0:T(128)S(1)} %get-tuple-element.87, f32[64]{0:T(128)S(1)} %get-tuple-element.88, f32[64]{0:T(128)S(1)} %get-tuple-element.86, f32[64]{0:T(128)S(1)} %get-tuple-element.93), kind=kLoop, calls=%fused_computation.24 | loop fusion | flops 3784704 | bytes 10814464 | tf_op jit(solution)/shard_map/add | solution.py:65
  316.6 4.9 %fusion.157 = (f32[64,2,128]{1,2,0:T(8,128)}, f32[64,2,128]{1,2,0:T(8,128)}) fusion(f32[64,64,128]{1,2,0:T(8,128)S(1)} %fusion.28), kind=kLoop, calls=%fused_computation.470 | loop fusion | bytes 262144 | tf_op jit(solution)/shard_map/slice | solution.py:11
  321.5 2.8 copy.36
  324.4 2.8 copy.37
  327.2 4.7 %collective-permute-start.13 = (f32[64,2,128]{2,0,1:T(8,128)S(1)}, f32[64,2,128]{2,0,1:T(8,128)S(1)}, u32[]{:S(2)}, u32[]{:S(2)}) collective-permute-start(f32[64,2,128]{2,0,1:T(8,128)S(1)} %copy.37), channel_id=1, source_target_pairs={{4,0},{8,4},{12,8},{16,12},{20,16},{24,20},{28,24},{0,28},{5,1},{9... | collective-permute-start | bytes 196616 | tf_op jit(solution)/shard_map/ppermute | solution.py:16
  343.2 3.8 pad_maximum_fusion.3
  347.0 5.1 %gather_fusion.12 = f32[64,68,132]{1,2,0:T(8,128)} fusion(f32[64,68,132]{1,2,0:T(8,128)} %pad_maximum_fusion.3, s32[1024]{0:T(1024)S(1)} %get-tuple-element.157), kind=kCustom, calls=%fused_computation.12.clone | custom fusion | bytes 4595968 | tf_op jit(solution)/shard_map/jit(_take)/gather | solution.py:62
  352.1 5.2 %gather_fusion.13 = f32[64,68,132]{1,2,0:T(8,128)} fusion(f32[64,68,132]{1,2,0:T(8,128)} %pad_maximum_fusion.3, s32[1024]{0:T(1024)S(1)} %get-tuple-element.156), kind=kCustom, calls=%fused_computation.13.clone | custom fusion | bytes 4595968 | tf_op jit(solution)/shard_map/jit(_take)/gather | solution.py:62
  357.4 5.2 %gather_fusion.14 = f32[64,68,132]{1,2,0:T(8,128)} fusion(f32[64,68,132]{1,2,0:T(8,128)} %pad_maximum_fusion.3, s32[1024]{0:T(1024)S(1)} %get-tuple-element.155), kind=kCustom, calls=%fused_computation.14.clone | custom fusion | bytes 4595968 | tf_op jit(solution)/shard_map/jit(_take)/gather | solution.py:62
  362.6 5.2 %gather_fusion.15 = f32[64,68,132]{1,2,0:T(8,128)} fusion(f32[64,68,132]{1,2,0:T(8,128)} %pad_maximum_fusion.3, s32[1024]{0:T(1024)S(1)} %get-tuple-element.154), kind=kCustom, calls=%fused_computation.15.clone | custom fusion | bytes 4595968 | tf_op jit(solution)/shard_map/jit(_take)/gather | solution.py:62
  367.9 7.3 %fusion.12 = f32[64,68,132]{1,2,0:T(8,128)S(1)} fusion(f32[64,68,132]{1,2,0:T(8,128)} %gather_fusion.15, f32[64,68,132]{1,2,0:T(8,128)} %gather_fusion.14, f32[64,68,132]{1,2,0:T(8,128)} %gather_fusion.13, f32[64,68,132]{1,2,0:T(8,128)} %gather_fusion.12, f32[64]{0:T(128)S(1)} %copy-done.25, f32[64]{0:T(128)S(1)} %copy-done.26, f32[64]{0:T(128)S(1)} %copy-done.24, ...), kind=kLoop, calls=%fused_computation.49 | loop fusion | flops 6319104 | bytes 11490560 | tf_op jit(solution)/shard_map/add | solution.py:62
  375.3 4.5 %fusion = f32[64,64,132]{1,2,0:T(8,128)S(1)} fusion(f32[64,68,132]{1,2,0:T(8,128)S(1)} %fusion.12, f32[64]{0:T(128)S(1)} %copy-done.33, f32[64]{0:T(128)S(1)} %copy-done.34, f32[64]{0:T(128)S(1)} %copy-done.32, f32[64]{0:T(128)S(1)} %copy-done.35), kind=kLoop, calls=%fused_computation.17 | loop fusion | flops 3784704 | bytes 10814464 | tf_op jit(solution)/shard_map/add | solution.py:65
  379.8 3.6 fusion.25
  386.2 54.7 %all_to_all.36 = f32[64,128,64]{1,2,0:T(8,128)S(1)} all-to-all(f32[64,128,64]{1,2,0:T(8,128)S(1)} %copy.40), channel_id=1, replica_groups=mesh['gz'=8,'xy'=4] {'gz'}, dimensions={0} | all-to-all | bytes 4194304 | tf_op jit(solution)/shard_map/all_to_all | solution.py:70
  (157 shorter events, 71.0 us)
Async XLA Ops:
  0.0 109.7 %copy-start = (f32[16,3]{0,1:T(4,128)S(1)}, f32[16,3]{0,1:T(4,128)}, u32[]{:S(2)}) copy-start(f32[16,3]{0,1:T(4,128)} %param.9) | copy-start | bytes 580
  0.0 10.2 %copy-start.18 = (s32[4,8,1,4]{1,3,2,0:T(4,128)S(1)}, s32[4,8,1,4]{1,3,2,0:T(4,128)}, u32[]{:S(2)}) copy-start(s32[4,8,1,4]{1,3,2,0:T(4,128)} %param.8) | copy-start | bytes 1540
  0.0 10.4 %copy-start.19 = (s32[4,8,1,4]{1,3,2,0:T(4,128)S(1)}, s32[4,8,1,4]{1,3,2,0:T(4,128)}, u32[]{:S(2)}) copy-start(s32[4,8,1,4]{1,3,2,0:T(4,128)} %param.7) | copy-start | bytes 1540
  2.9 109.0 %all-to-all-start = ((f32[8,128,512]{1,0,2:T(8,128)}), f32[8,128,512]{1,0,2:T(8,128)S(1)}, u32[]{:S(2)}, u32[]{:S(2)}) async-start(f32[8,128,512]{1,0,2:T(8,128)} %copy.20), calls=%async_computation | async-start | bytes 4194304 | tf_op jit(solution)/shard_map/all_to_all | solution.py:39
  128.9 7.7 %collective-permute-start = (f32[64,2,128]{2,0,1:T(8,128)S(1)}, f32[64,2,128]{2,0,1:T(8,128)S(1)}, u32[]{:S(2)}, u32[]{:S(2)}) collective-permute-start(f32[64,2,128]{2,0,1:T(8,128)S(1)} %copy.24), channel_id=1, source_target_pairs={{0,4},{4,8},{8,12},{12,16},{16,20},{20,24},{24,28},{28,0},{1,5},{5... | collective-permute-start | bytes 196616 | tf_op jit(solution)/shard_map/ppermute | solution.py:14
  131.8 7.5 %collective-permute-start.1 = (f32[64,2,128]{2,0,1:T(8,128)S(1)}, f32[64,2,128]{2,0,1:T(8,128)S(1)}, u32[]{:S(2)}, u32[]{:S(2)}) collective-permute-start(f32[64,2,128]{2,0,1:T(8,128)S(1)} %copy.25), channel_id=1, source_target_pairs={{4,0},{8,4},{12,8},{16,12},{20,16},{24,20},{28,24},{0,28},{5,1},{9... | collective-permute-start | bytes 196616 | tf_op jit(solution)/shard_map/ppermute | solution.py:16
  141.9 5.7 %copy-start.2 = (f32[64,128,64]{2,1,0:T(8,128)S(1)}, f32[64,128,64]{2,1,0:T(8,128)}, u32[]{:S(2)}) copy-start(f32[64,128,64]{2,1,0:T(8,128)} %copy.23) | copy-start | bytes 6291460
  141.9 5.7 %copy-start.9 = (f32[64,2,128]{1,2,0:T(8,128)S(1)}, f32[64,2,128]{1,2,0:T(8,128)}, u32[]{:S(2)}) copy-start(f32[64,2,128]{1,2,0:T(8,128)} %copy.26) | copy-start | bytes 196612
  141.9 5.7 %copy-start.13 = (f32[64,2,128]{1,2,0:T(8,128)S(1)}, f32[64,2,128]{1,2,0:T(8,128)}, u32[]{:S(2)}) copy-start(f32[64,2,128]{1,2,0:T(8,128)} %copy.27) | copy-start | bytes 196612
  143.8 3.7 collective-permute-start.2
  143.8 3.8 collective-permute-start.3
  186.2 4.9 %copy-start.3 = (f32[64,64,128]{1,2,0:T(8,128)}, f32[64,64,128]{1,2,0:T(8,128)S(1)}, u32[]{:S(2)}) copy-start(f32[64,64,128]{1,2,0:T(8,128)S(1)} %fusion.34) | copy-start | bytes 6291460
  193.9 7.7 %collective-permute-start.4 = (f32[64,2,128]{2,0,1:T(8,128)S(1)}, f32[64,2,128]{2,0,1:T(8,128)S(1)}, u32[]{:S(2)}, u32[]{:S(2)}) collective-permute-start(f32[64,2,128]{2,0,1:T(8,128)S(1)} %copy.28), channel_id=1, source_target_pairs={{0,4},{4,8},{8,12},{12,16},{16,20},{20,24},{24,28},{28,0},{1,5},{5... | collective-permute-start | bytes 196616 | tf_op jit(solution)/shard_map/ppermute | solution.py:14
  196.8 7.5 %collective-permute-start.5 = (f32[64,2,128]{2,0,1:T(8,128)S(1)}, f32[64,2,128]{2,0,1:T(8,128)S(1)}, u32[]{:S(2)}, u32[]{:S(2)}) collective-permute-start(f32[64,2,128]{2,0,1:T(8,128)S(1)} %copy.29), channel_id=1, source_target_pairs={{4,0},{8,4},{12,8},{16,12},{20,16},{24,20},{28,24},{0,28},{5,1},{9... | collective-permute-start | bytes 196616 | tf_op jit(solution)/shard_map/ppermute | solution.py:16
  207.0 5.8 %copy-start.4 = (f32[64,64,128]{1,2,0:T(8,128)S(1)}, f32[64,64,128]{1,2,0:T(8,128)}, u32[]{:S(2)}) copy-start(f32[64,64,128]{1,2,0:T(8,128)} %copy-done.3) | copy-start | bytes 6291460
  207.0 5.8 %copy-start.10 = (f32[64,2,128]{1,2,0:T(8,128)S(1)}, f32[64,2,128]{1,2,0:T(8,128)}, u32[]{:S(2)}) copy-start(f32[64,2,128]{1,2,0:T(8,128)} %copy.30) | copy-start | bytes 196612
  207.0 5.8 %copy-start.14 = (f32[64,2,128]{1,2,0:T(8,128)S(1)}, f32[64,2,128]{1,2,0:T(8,128)}, u32[]{:S(2)}) copy-start(f32[64,2,128]{1,2,0:T(8,128)} %copy.31) | copy-start | bytes 196612
  208.9 3.7 collective-permute-start.6
  210.0 2.8 collective-permute-start.7
  259.0 7.7 %collective-permute-start.8 = (f32[64,2,128]{2,0,1:T(8,128)S(1)}, f32[64,2,128]{2,0,1:T(8,128)S(1)}, u32[]{:S(2)}, u32[]{:S(2)}) collective-permute-start(f32[64,2,128]{2,0,1:T(8,128)S(1)} %copy.32), channel_id=1, source_target_pairs={{0,4},{4,8},{8,12},{12,16},{16,20},{20,24},{24,28},{28,0},{1,5},{5... | collective-permute-start | bytes 196616 | tf_op jit(solution)/shard_map/ppermute | solution.py:14
  261.9 7.5 %collective-permute-start.9 = (f32[64,2,128]{2,0,1:T(8,128)S(1)}, f32[64,2,128]{2,0,1:T(8,128)S(1)}, u32[]{:S(2)}, u32[]{:S(2)}) collective-permute-start(f32[64,2,128]{2,0,1:T(8,128)S(1)} %copy.33), channel_id=1, source_target_pairs={{4,0},{8,4},{12,8},{16,12},{20,16},{24,20},{28,24},{0,28},{5,1},{9... | collective-permute-start | bytes 196616 | tf_op jit(solution)/shard_map/ppermute | solution.py:16
  272.1 6.0 %copy-start.6 = (f32[64,64,128]{1,2,0:T(8,128)S(1)}, f32[64,64,128]{1,2,0:T(8,128)}, u32[]{:S(2)}) copy-start(f32[64,64,128]{1,2,0:T(8,128)} %copy-done.5) | copy-start | bytes 6291460
  272.1 6.0 %copy-start.11 = (f32[64,2,128]{1,2,0:T(8,128)S(1)}, f32[64,2,128]{1,2,0:T(8,128)}, u32[]{:S(2)}) copy-start(f32[64,2,128]{1,2,0:T(8,128)} %copy.34) | copy-start | bytes 196612
  272.1 6.0 %copy-start.15 = (f32[64,2,128]{1,2,0:T(8,128)S(1)}, f32[64,2,128]{1,2,0:T(8,128)}, u32[]{:S(2)}) copy-start(f32[64,2,128]{1,2,0:T(8,128)} %copy.35) | copy-start | bytes 196612
  274.0 3.7 collective-permute-start.10
  275.1 3.0 collective-permute-start.11
  321.5 10.5 %copy-start.38 = (s32[64]{0:T(128)S(1)}, s32[64]{0:T(128)}, u32[]{:S(2)}) copy-start(s32[64]{0:T(128)} %get-tuple-element.15) | copy-start | bytes 772
  321.5 10.5 %copy-start.39 = (s32[64]{0:T(128)S(1)}, s32[64]{0:T(128)}, u32[]{:S(2)}) copy-start(s32[64]{0:T(128)} %get-tuple-element.119) | copy-start | bytes 772
  324.3 7.7 %collective-permute-start.12 = (f32[64,2,128]{2,0,1:T(8,128)S(1)}, f32[64,2,128]{2,0,1:T(8,128)S(1)}, u32[]{:S(2)}, u32[]{:S(2)}) collective-permute-start(f32[64,2,128]{2,0,1:T(8,128)S(1)} %copy.36), channel_id=1, source_target_pairs={{0,4},{4,8},{8,12},{12,16},{16,20},{20,24},{24,28},{28,0},{1,5},{5... | collective-permute-start | bytes 196616 | tf_op jit(solution)/shard_map/ppermute | solution.py:14
  327.2 7.5 %collective-permute-start.13 = (f32[64,2,128]{2,0,1:T(8,128)S(1)}, f32[64,2,128]{2,0,1:T(8,128)S(1)}, u32[]{:S(2)}, u32[]{:S(2)}) collective-permute-start(f32[64,2,128]{2,0,1:T(8,128)S(1)} %copy.37), channel_id=1, source_target_pairs={{4,0},{8,4},{12,8},{16,12},{20,16},{24,20},{28,24},{0,28},{5,1},{9... | collective-permute-start | bytes 196616 | tf_op jit(solution)/shard_map/ppermute | solution.py:16
  337.4 5.7 %copy-start.8 = (f32[64,64,128]{1,2,0:T(8,128)S(1)}, f32[64,64,128]{1,2,0:T(8,128)}, u32[]{:S(2)}) copy-start(f32[64,64,128]{1,2,0:T(8,128)} %copy-done.7) | copy-start | bytes 6291460
  337.4 5.7 %copy-start.12 = (f32[64,2,128]{1,2,0:T(8,128)S(1)}, f32[64,2,128]{1,2,0:T(8,128)}, u32[]{:S(2)}) copy-start(f32[64,2,128]{1,2,0:T(8,128)} %copy.38) | copy-start | bytes 196612
  337.4 5.7 %copy-start.16 = (f32[64,2,128]{1,2,0:T(8,128)S(1)}, f32[64,2,128]{1,2,0:T(8,128)}, u32[]{:S(2)}) copy-start(f32[64,2,128]{1,2,0:T(8,128)} %copy.39) | copy-start | bytes 196612
  339.3 3.7 collective-permute-start.14
  340.5 2.6 collective-permute-start.15
  362.6 5.2 %copy-start.20 = (pred[64]{0:T(512)(128)(4,1)S(1)}, pred[64]{0:T(512)(128)(4,1)}, u32[]{:S(2)}) copy-start(pred[64]{0:T(512)(128)(4,1)} %get-tuple-element.14) | copy-start | bytes 196
  362.6 5.2 %copy-start.21 = (pred[64]{0:T(512)(128)(4,1)S(1)}, pred[64]{0:T(512)(128)(4,1)}, u32[]{:S(2)}) copy-start(pred[64]{0:T(512)(128)(4,1)} %get-tuple-element.118) | copy-start | bytes 196
  362.6 5.2 %copy-start.22 = (pred[64]{0:T(512)(128)(4,1)S(1)}, pred[64]{0:T(512)(128)(4,1)}, u32[]{:S(2)}) copy-start(pred[64]{0:T(512)(128)(4,1)} %get-tuple-element.120) | copy-start | bytes 196
  362.6 5.2 %copy-start.23 = (pred[64]{0:T(512)(128)(4,1)S(1)}, pred[64]{0:T(512)(128)(4,1)}, u32[]{:S(2)}) copy-start(pred[64]{0:T(512)(128)(4,1)} %get-tuple-element.122) | copy-start | bytes 196
  362.6 5.2 %copy-start.24 = (f32[64]{0:T(128)S(1)}, f32[64]{0:T(128)}, u32[]{:S(2)}) copy-start(f32[64]{0:T(128)} %get-tuple-element.77) | copy-start | bytes 772
  362.6 5.2 %copy-start.25 = (f32[64]{0:T(128)S(1)}, f32[64]{0:T(128)}, u32[]{:S(2)}) copy-start(f32[64]{0:T(128)} %get-tuple-element.78) | copy-start | bytes 772
  362.6 5.2 %copy-start.26 = (f32[64]{0:T(128)S(1)}, f32[64]{0:T(128)}, u32[]{:S(2)}) copy-start(f32[64]{0:T(128)} %get-tuple-element.79) | copy-start | bytes 772
  362.6 5.2 %copy-start.27 = (f32[64]{0:T(128)S(1)}, f32[64]{0:T(128)}, u32[]{:S(2)}) copy-start(f32[64]{0:T(128)} %get-tuple-element.80) | copy-start | bytes 772
  367.9 7.3 %copy-start.32 = (f32[64]{0:T(128)S(1)}, f32[64]{0:T(128)}, u32[]{:S(2)}) copy-start(f32[64]{0:T(128)} %get-tuple-element.74) | copy-start | bytes 772
  367.9 7.3 %copy-start.33 = (f32[64]{0:T(128)S(1)}, f32[64]{0:T(128)}, u32[]{:S(2)}) copy-start(f32[64]{0:T(128)} %get-tuple-element.75) | copy-start | bytes 772
  367.9 7.3 %copy-start.34 = (f32[64]{0:T(128)S(1)}, f32[64]{0:T(128)}, u32[]{:S(2)}) copy-start(f32[64]{0:T(128)} %get-tuple-element.76) | copy-start | bytes 772
  367.9 7.3 %copy-start.35 = (f32[64]{0:T(128)S(1)}, f32[64]{0:T(128)}, u32[]{:S(2)}) copy-start(f32[64]{0:T(128)} %get-tuple-element.81) | copy-start | bytes 772
  386.2 56.7 %copy-start.1 = (f32[16,3]{0,1:T(4,128)S(1)}, f32[16,3]{0,1:T(4,128)}, u32[]{:S(2)}) copy-start(f32[16,3]{0,1:T(4,128)} %param.9) | copy-start | bytes 580
  (9 other events, 36.8 us)
where the time goes:
time: 449 us; the launch traced here: 443 us
  local copies, waits for them, and re-layouts  164 us (37%)
  blocking collectives  153 us (34%)
  other arithmetic  81.6 us (18%)
  starting transfers between devices  34.5 us (8%)
  waiting for transfers between devices  7.61 us (2%)
    gather x16, local copies, waits for them, and re-layouts, column_steps(): jnp.take(rimmed, source, axis=0)  83.1 us
    all_gather x1, blocking collectives, column_steps(): lax.all_gather(frac_index, 'gz', axis=1, tiled=True)  68.2 us
    all_to_all x1, blocking collectives, column_steps(): lax.all_to_all(jnp.swapaxes(standing, 1, 2), 'gz', split_axis=0, concat_a...  54.7 us
    slice x8, local copies, waits for them, and re-layouts, extended(): lax.slice_in_dim(cells, cells.shape[dim] - width, cells.shape[dim], axis=...  34 us
    all_gather x1, blocking collectives, column_steps(): lax.all_gather(offsets, 'gz', axis=1, tiled=True)  30.5 us
    add x4, other arithmetic, column_steps(): merged + zweights[node][:, None, None] * jnp.take(rimmed, source, axis=0)  29 us
    ppermute x8, starting transfers between devices, extended(): lax.ppermute(head, axis, [((i + 1) % count, i) for i in range(count)])  23.5 us
    add x4, other arithmetic, column_steps(): along_y + yweights[node][:, None, None] * merged[:, node:node + width_y, :]  17.9 us
  transfers between devices with their start and end apart: 17, of which 8 were waited for; matrix products, arithmetic and copies ran while one was open for 6% of the time, Pallas kernels for 0%

commit v1 on v0

--- a/solution.py
+++ b/solution.py
@@ -1,7 +1,255 @@
+import functools
+
 import jax
 import jax.numpy as jnp
 from jax import lax
+from jax.experimental import pallas as pl
+from jax.experimental.pallas import tpu as pltpu
 from jax.sharding import PartitionSpec as P
+
+MESH = pl.DeviceIdType.MESH
+LANES = 128
+
+
+def slot_of(g, n):
+    if n % 2:
+        return g
+    far, near = g // 2, g % 2
+    return far + near * (n - 1 - 2 * far)
+
+
+def device_at(slot, n):
+    if n % 2:
+        return slot
+    half = slot // (n // 2)
+    return 2 * (slot + half * (n - 1 - 2 * slot)) + half
+
+
+def fused_kernel(
+    n, n_xy, steps, order,
+    image_ref, meta_ref, table_ref, out_ref, meta_all_ref,
+    landed, cells_a, cells_b, final, send_high, send_low, recv_high, recv_low, meta_s,
+    in_send, in_recv, meta_send, meta_recv, halo_send, halo_recv, out_send, out_recv, local_sem,
+):
+    planes = image_ref.shape[0]
+    nz = n * planes
+    rows = final.shape[1]
+    blocks = final.shape[2] // LANES
+    me = lax.axis_index("gz")
+    xy = lax.axis_index("xy")
+    slot = slot_of(me, n)
+    line = xy * n + slot
+    after = lax.rem(line + 1, n * n_xy)
+    before = lax.rem(line + n * n_xy - 1, n * n_xy)
+    next_id = (device_at(lax.rem(after, n), n), after // n)
+    prev_id = (device_at(lax.rem(before, n), n), before // n)
+
+    barrier = pltpu.get_barrier_semaphore()
+    for i in range(1, n):
+        pl.semaphore_signal(barrier, inc=1, device_id=(lax.rem(me + i, n), xy), device_id_type=MESH)
+    for neighbour in (next_id, prev_id):
+        pl.semaphore_signal(barrier, inc=1, device_id=neighbour, device_id_type=MESH)
+    pl.semaphore_wait(barrier, n + 1)
+
+    def meta_copy(i, owner, to):
+        return pltpu.make_async_remote_copy(
+            src_ref=meta_ref, dst_ref=meta_all_ref.at[pl.ds(pl.multiple_of(owner * 8, 8), 8)],
+            send_sem=meta_send.at[i], recv_sem=meta_recv.at[i], device_id=(to, xy), device_id_type=MESH)
+
+    def in_copy(i, owner, to):
+        return pltpu.make_async_remote_copy(
+            src_ref=image_ref.at[:, pl.ds(pl.multiple_of(slot_of(to, n) * rows, 8), rows)],
+            dst_ref=landed.at[pl.ds(owner * planes, planes)],
+            send_sem=in_send.at[i], recv_sem=in_recv.at[i], device_id=(to, xy), device_id_type=MESH)
+
+    def out_copy(i, to, owner_slot):
+        return pltpu.make_async_remote_copy(
+            src_ref=final.at[pl.ds(to * planes, planes)],
+            dst_ref=out_ref.at[:, pl.ds(pl.multiple_of(owner_slot * rows, 8), rows)],
+            send_sem=out_send.at[i], recv_sem=out_recv.at[i], device_id=(to, xy), device_id_type=MESH)
+
+    for i in order:
+        to = lax.rem(me + i, n)
+        meta_copy(i, me, to).start()
+        in_copy(i, me, to).start()
+    own_meta = pltpu.make_async_copy(
+        meta_ref, meta_all_ref.at[pl.ds(pl.multiple_of(me * 8, 8), 8)], local_sem.at[0])
+    own_in = pltpu.make_async_copy(
+        image_ref.at[:, pl.ds(pl.multiple_of(slot * rows, 8), rows)],
+        landed.at[pl.ds(me * planes, planes)], local_sem.at[1])
+    own_meta.start()
+    own_in.start()
+    own_meta.wait()
+    for i in order:
+        meta_copy(i, lax.rem(me - i + n, n), lax.rem(me + i, n)).wait()
+    to_scalar = pltpu.make_async_copy(meta_all_ref, meta_s, local_sem.at[2])
+    to_scalar.start()
+    to_scalar.wait()
+    own_in.wait()
+    for i in order:
+        in_copy(i, lax.rem(me - i + n, n), lax.rem(me + i, n)).wait()
+
+    def halo_copies(s, group):
+        part = pl.ds(group * planes, planes)
+        return (
+            pltpu.make_async_remote_copy(
+                src_ref=send_high.at[s, part], dst_ref=recv_high.at[s, part],
+                send_sem=halo_send.at[s, 0, group], recv_sem=halo_recv.at[s, 0, group],
+                device_id=next_id, device_id_type=MESH),
+            pltpu.make_async_remote_copy(
+                src_ref=send_low.at[s, part], dst_ref=recv_low.at[s, part],
+                send_sem=halo_send.at[s, 1, group], recv_sem=halo_recv.at[s, 1, group],
+                device_id=prev_id, device_id_type=MESH),
+        )
+
+    def edges(s, k, b, value):
+        send_high[s, k, pl.ds(2 * b, 2), :] = value[rows - 2 : rows]
+        send_low[s, k, pl.ds(b, 1), :] = value[0:1]
+
+    @pl.loop(0, n)
+    def _(group):
+        @pl.loop(0, planes)
+        def _(inner):
+            k = group * planes + inner
+            for b in range(blocks):
+                value = landed[k, :, pl.ds(b * LANES, LANES)]
+                cells_a[k, b, pl.ds(2, rows), :] = value
+                edges(0, k, b, value)
+        for copy in halo_copies(0, group):
+            copy.start()
+
+    tall = cells_a.shape[2]
+    lane = lax.broadcasted_iota(jnp.int32, (tall, LANES), 1)
+    left = lane >= LANES // 2
+    last_two = lane >= LANES - 2
+    last_one = lane >= LANES - 1
+    first = lane < 1
+
+    for s in range(steps):
+        source, target = (cells_a, cells_b) if s % 2 == 0 else (cells_b, cells_a)
+
+        @pl.loop(0, n)
+        def _(group):
+            for copy in halo_copies(s, group):
+                copy.wait()
+
+        @pl.loop(0, nz)
+        def _(k):
+            for b in range(blocks):
+                source[k, b, pl.ds(0, 2), :] = recv_high[s, k, pl.ds(2 * b, 2), :]
+                source[k, b, pl.ds(rows + 2, 1), :] = recv_low[s, k, pl.ds(b, 1), :]
+
+        def plane(group, inner):
+            k = group * planes + inner
+            for b in range(blocks):
+                spot = (s * planes + inner) * blocks + b
+                shift = meta_s[group * 8, spot]
+                row = meta_s[group * 8 + 1, spot]
+                weight = [table_ref[row, j] for j in range(12)]
+                merged = None
+                rim = None
+                for node in range(4):
+                    at = k - shift - 2 + node + 2 * nz
+                    at = jnp.bitwise_and(at, nz - 1) if nz & (nz - 1) == 0 else lax.rem(at, nz)
+                    own = weight[node] * source[at, b]
+                    side = weight[node] * jnp.where(
+                        left, source[at, (b - 1) % blocks], source[at, (b + 1) % blocks])
+                    merged = own if merged is None else merged + own
+                    rim = side if rim is None else rim + side
+                along = (
+                    weight[8] * pltpu.roll(jnp.where(last_two, rim, merged), 2, 1)
+                    + weight[9] * pltpu.roll(jnp.where(last_one, rim, merged), 1, 1)
+                    + weight[10] * merged
+                    + weight[11] * pltpu.roll(jnp.where(first, rim, merged), LANES - 1, 1)
+                )
+                value = weight[4] * along[0:rows]
+                for node in range(1, 4):
+                    value = value + weight[4 + node] * along[node : node + rows]
+                if s < steps - 1:
+                    target[k, b, pl.ds(2, rows), :] = value
+                    edges(s + 1, k, b, value)
+                else:
+                    final[k, :, pl.ds(b * LANES, LANES)] = value
+
+        if s < steps - 1:
+            @pl.loop(0, n)
+            def _(group):
+                @pl.loop(0, planes)
+                def _(inner):
+                    plane(group, inner)
+                for copy in halo_copies(s + 1, group):
+                    copy.start()
+        else:
+            @pl.loop(1, n)
+            def _(i):
+                to = lax.rem(me + i, n)
+                @pl.loop(0, planes)
+                def _(inner):
+                    plane(to, inner)
+                out_copy(i, to, slot).start()
+            @pl.loop(0, planes)
+            def _(inner):
+                plane(me, inner)
+
+    own_out = pltpu.make_async_copy(
+        final.at[pl.ds(me * planes, planes)],
+        out_ref.at[:, pl.ds(pl.multiple_of(slot * rows, 8), rows)], local_sem.at[3])
+    own_out.start()
+    own_out.wait()
+    for i in range(1, n):
+        out_copy(i, lax.rem(me + i, n), slot_of(lax.rem(me - i + n, n), n)).wait()
+
+
+def fused(image, offsets, frac_index, fractions, n, n_xy):
+    planes, width, depth = image.shape
+    steps, blocks = offsets.shape[0], offsets.shape[3]
+    rows = width // n
+    nz = n * planes
+    length = steps * planes * blocks
+    padded = -(-length // LANES) * LANES
+    meta = jnp.stack([offsets.reshape(length), frac_index.reshape(length)])
+    meta = jnp.pad(meta, ((0, 6), (0, padded - length)))
+    columns = []
+    for axis in range(3):
+        columns.extend(cubic_weights(1.0 - fractions[:, axis]))
+    table = jnp.stack(columns, axis=1)
+    tall = -(-(rows + 3) // 8) * 8
+    out, _ = pl.pallas_call(
+        functools.partial(fused_kernel, n, n_xy, steps, tuple(range(1, n))),
+        out_shape=(
+            jax.ShapeDtypeStruct(image.shape, jnp.float32),
+            jax.ShapeDtypeStruct((n * 8, padded), jnp.int32),
+        ),
+        in_specs=[
+            pl.BlockSpec(memory_space=pl.ANY),
+            pl.BlockSpec(memory_space=pl.ANY),
+            pl.BlockSpec(memory_space=pltpu.SMEM),
+        ],
+        out_specs=(pl.BlockSpec(memory_space=pl.ANY), pl.BlockSpec(memory_space=pl.ANY)),
+        scratch_shapes=[
+            pltpu.VMEM((nz, rows, depth), jnp.float32),
+            pltpu.VMEM((nz, blocks, tall, LANES), jnp.float32),
+            pltpu.VMEM((nz, blocks, tall, LANES), jnp.float32),
+            pltpu.VMEM((nz, rows, depth), jnp.float32),
+            pltpu.VMEM((steps, nz, 2 * blocks, LANES), jnp.float32),
+            pltpu.VMEM((steps, nz, blocks, LANES), jnp.float32),
+            pltpu.VMEM((steps, nz, 2 * blocks, LANES), jnp.float32),
+            pltpu.VMEM((steps, nz, blocks, LANES), jnp.float32),
+            pltpu.SMEM((n * 8, padded), jnp.int32),
+            pltpu.SemaphoreType.DMA((n,)),
+            pltpu.SemaphoreType.DMA((n,)),
+            pltpu.SemaphoreType.DMA((n,)),
+            pltpu.SemaphoreType.DMA((n,)),
+            pltpu.SemaphoreType.DMA((steps, 2, n)),
+            pltpu.SemaphoreType.DMA((steps, 2, n)),
+            pltpu.SemaphoreType.DMA((n,)),
+            pltpu.SemaphoreType.DMA((n,)),
+            pltpu.SemaphoreType.DMA((4,)),
+        ],
+        compiler_params=pltpu.CompilerParams(
+            collective_id=0, has_side_effects=True, vmem_limit_bytes=48 * 1024 * 1024),
+    )(image, meta, table)
+    return out
 
 
 def extended(cells, sides, width):
@@ -72,11 +320,16 @@
     )
 
 
-def local(image, offsets, frac_index, fractions):
-    return column_steps(image, offsets, frac_index, fractions)
-
-
 def solution(mesh):
+    n, n_xy = mesh.shape["gz"], mesh.shape["xy"]
+
+    def local(image, offsets, frac_index, fractions):
+        planes, width, depth = image.shape
+        block = depth // offsets.shape[3]
+        if block == width == LANES and offsets.shape[2] == 1 and width % (8 * n) == 0 and n > 1:
+            return fused(image, offsets, frac_index, fractions, n, n_xy)
+        return column_steps(image, offsets, frac_index, fractions)
+
     in_specs = (P("gz", "xy", None), P(None, "gz", "xy", None), P(None, "gz", "xy", None), P())
     out_specs = P("gz", "xy", None)
     return jax.shard_map(local, mesh=mesh, in_specs=in_specs, out_specs=out_specs, check_vma=False)

time: 449 us -> 153 us (0.34)
  the two profiles are of different devices: /device:TPU:0 before, /device:TPU:15 now
where the time goes in v1:
time: 153 us; the launch traced here: 152 us
  Pallas kernels  146 us (95%)
  local copies, waits for them, and re-layouts  5.84 us (4%)
    pallas_call x1, Pallas kernels, fused(): pl.pallas_call(functools.partial(fused_kernel, n, n_xy, steps, tuple(rang...  146 us
    unnamed x8, local copies, waits for them, and re-layouts  4.74 us

profile of v1, /device:TPU:15, one launch (start us, length us, event | category | flops | bytes accessed | tf_op | source)
XLA Modules:
  0.0 151.8 jit_solution(13488572305343624636)
XLA Ops:
  0.0 0.8 fusion
  0.8 0.1 copy.25
  0.9 0.1 copy.24
  1.0 0.1 copy.23
  1.0 0.8 copy.15
  1.8 0.1 stack_reshape.6
  1.9 0.8 copy.16
  2.7 0.1 stack_reshape.7
  2.9 0.1 stack.5.table_ref
  3.0 0.0 copy-start
  3.0 1.6 %copy-done = f32[8,128,512]{2,1,0:T(8,128)S(1)} copy-done((f32[8,128,512]{2,1,0:T(8,128)S(1)}, f32[8,128,512]{2,1,0:T(8,128)}, u32[]{:S(2)}) %copy-start) | copy-done | bytes 2097176
  4.6 145.8 %shard_map.46 = (f32[8,128,512]{2,1,0:T(8,128)S(1)}, s32[64,128]{1,0:T(8,128)}) custom-call(f32[8,128,512]{2,1,0:T(8,128)S(1)} %copy-done, s32[8,128]{1,0:T(8,128)S(1)} %pad.4.meta_ref, f32[16,12]{1,0:T(8,128)S(1)} %stack.5.table_ref), custom_call_target="tpu_custom_call" | custom-call | tf_op jit(solution)/shard_map/pallas_call | solution.py:217
  150.4 1.3 copy.27
  (4 shorter events, 0.0 us)
Async XLA Ops:
  3.0 1.6 %copy-start = (f32[8,128,512]{2,1,0:T(8,128)S(1)}, f32[8,128,512]{2,1,0:T(8,128)}, u32[]{:S(2)}) copy-start(f32[8,128,512]{2,1,0:T(8,128)} %image_ref.1) | copy-start | bytes 6291460

commit v2 on v1

--- a/solution.py
+++ b/solution.py
@@ -11,14 +11,15 @@
 LANES = 128
 
 
-def slot_of(g, n):
-    if n % 2:
-        return g
-    far, near = g // 2, g % 2
-    return far + near * (n - 1 - 2 * far)
-
-
-def device_at(slot, n):
+def slot_of(g, n, strip):
+    if n % 2 == 0:
+        far, near = g // 2, g % 2
+        g = far + near * (n - 1 - 2 * far)
+    return g + (strip % 2) * (n - 1 - 2 * g)
+
+
+def device_at(slot, n, strip):
+    slot = slot + (strip % 2) * (n - 1 - 2 * slot)
     if n % 2:
         return slot
     half = slot // (n // 2)
@@ -26,7 +27,7 @@
 
 
 def fused_kernel(
-    n, n_xy, steps, order,
+    n, n_xy, steps,
     image_ref, meta_ref, table_ref, out_ref, meta_all_ref,
     landed, cells_a, cells_b, final, send_high, send_low, recv_high, recv_low, meta_s,
     in_send, in_recv, meta_send, meta_recv, halo_send, halo_recv, out_send, out_recv, local_sem,
@@ -35,69 +36,102 @@
     nz = n * planes
     rows = final.shape[1]
     blocks = final.shape[2] // LANES
+    pair = 2 if n_xy % 2 == 0 else 1
+    pieces = n * pair
     me = lax.axis_index("gz")
     xy = lax.axis_index("xy")
-    slot = slot_of(me, n)
-    line = xy * n + slot
-    after = lax.rem(line + 1, n * n_xy)
-    before = lax.rem(line + n * n_xy - 1, n * n_xy)
-    next_id = (device_at(lax.rem(after, n), n), after // n)
-    prev_id = (device_at(lax.rem(before, n), n), before // n)
+    strip, half = xy // pair, lax.rem(xy, pair)
+    piece = slot_of(me, n, strip) * pair + half
+    home = strip * pair + piece // n
+    part = lax.rem(piece, n)
+    is_home = home == xy
+
+    def holder(line):
+        strip_at, piece_at = line // pieces, lax.rem(line, pieces)
+        return (
+            device_at(piece_at // pair, n, strip_at),
+            strip_at * pair + lax.rem(piece_at, pair),
+        )
+
+    line = strip * pieces + piece
+    next_id = holder(lax.rem(line + 1, n * n_xy))
+    prev_id = holder(lax.rem(line + n * n_xy - 1, n * n_xy))
 
     barrier = pltpu.get_barrier_semaphore()
-    for i in range(1, n):
-        pl.semaphore_signal(barrier, inc=1, device_id=(lax.rem(me + i, n), xy), device_id_type=MESH)
+    for i in range(1, pieces):
+        other = lax.rem(half * n + me + i, pieces)
+        pl.semaphore_signal(
+            barrier, inc=1, device_id=(lax.rem(other, n), strip * pair + other // n), device_id_type=MESH)
     for neighbour in (next_id, prev_id):
         pl.semaphore_signal(barrier, inc=1, device_id=neighbour, device_id_type=MESH)
-    pl.semaphore_wait(barrier, n + 1)
-
-    def meta_copy(i, owner, to):
+    pl.semaphore_wait(barrier, pieces + 1)
+
+    def share(i):
+        return pl.ds(pl.multiple_of(i * rows, 8), rows)
+
+    def slab(g):
+        return pl.ds(g * planes, planes)
+
+    def eight(g):
+        return pl.ds(pl.multiple_of(g * 8, 8), 8)
+
+    def taker(i):
+        return holder(strip * pieces + half * n + i)
+
+    def meta_copy(i):
         return pltpu.make_async_remote_copy(
-            src_ref=meta_ref, dst_ref=meta_all_ref.at[pl.ds(pl.multiple_of(owner * 8, 8), 8)],
-            send_sem=meta_send.at[i], recv_sem=meta_recv.at[i], device_id=(to, xy), device_id_type=MESH)
-
-    def in_copy(i, owner, to):
+            src_ref=meta_ref, dst_ref=meta_all_ref.at[eight(me)],
+            send_sem=meta_send.at[i], recv_sem=meta_recv.at[me], device_id=taker(i), device_id_type=MESH)
+
+    def in_copy(i):
         return pltpu.make_async_remote_copy(
-            src_ref=image_ref.at[:, pl.ds(pl.multiple_of(slot_of(to, n) * rows, 8), rows)],
-            dst_ref=landed.at[pl.ds(owner * planes, planes)],
-            send_sem=in_send.at[i], recv_sem=in_recv.at[i], device_id=(to, xy), device_id_type=MESH)
-
-    def out_copy(i, to, owner_slot):
+            src_ref=image_ref.at[:, share(i)], dst_ref=landed.at[slab(me)],
+            send_sem=in_send.at[i], recv_sem=in_recv.at[me], device_id=taker(i), device_id_type=MESH)
+
+    def meta_wait(g):
+        return pltpu.make_async_copy(meta_ref, meta_all_ref.at[eight(g)], meta_recv.at[g])
+
+    def in_wait(g):
+        return pltpu.make_async_copy(image_ref.at[:, share(part)], landed.at[slab(g)], in_recv.at[g])
+
+    def out_copy(g):
         return pltpu.make_async_remote_copy(
-            src_ref=final.at[pl.ds(to * planes, planes)],
-            dst_ref=out_ref.at[:, pl.ds(pl.multiple_of(owner_slot * rows, 8), rows)],
-            send_sem=out_send.at[i], recv_sem=out_recv.at[i], device_id=(to, xy), device_id_type=MESH)
-
-    for i in order:
-        to = lax.rem(me + i, n)
-        meta_copy(i, me, to).start()
-        in_copy(i, me, to).start()
-    own_meta = pltpu.make_async_copy(
-        meta_ref, meta_all_ref.at[pl.ds(pl.multiple_of(me * 8, 8), 8)], local_sem.at[0])
-    own_in = pltpu.make_async_copy(
-        image_ref.at[:, pl.ds(pl.multiple_of(slot * rows, 8), rows)],
-        landed.at[pl.ds(me * planes, planes)], local_sem.at[1])
-    own_meta.start()
-    own_in.start()
-    own_meta.wait()
-    for i in order:
-        meta_copy(i, lax.rem(me - i + n, n), lax.rem(me + i, n)).wait()
-    to_scalar = pltpu.make_async_copy(meta_all_ref, meta_s, local_sem.at[2])
+            src_ref=final.at[slab(g)], dst_ref=out_ref.at[:, share(part)],
+            send_sem=out_send.at[g], recv_sem=out_recv.at[part], device_id=(g, home), device_id_type=MESH)
+
+    def out_wait(i):
+        return pltpu.make_async_copy(final.at[slab(me)], out_ref.at[:, share(i)], out_recv.at[i])
+
+    @pl.when(is_home)
+    def _():
+        meta_wait(me).start()
+        in_wait(me).start()
+
+    for make in (meta_copy, in_copy):
+        @pl.loop(0, n)
+        def _(turn):
+            i = lax.rem(turn + me, n)
+
+            @pl.when(jnp.logical_not(jnp.logical_and(is_home, i == part)))
+            def _():
+                make(i).start()
+
+    @pl.loop(0, n)
+    def _(g):
+        meta_wait(g).wait()
+    to_scalar = pltpu.make_async_copy(meta_all_ref, meta_s, local_sem.at[0])
     to_scalar.start()
     to_scalar.wait()
-    own_in.wait()
-    for i in order:
-        in_copy(i, lax.rem(me - i + n, n), lax.rem(me + i, n)).wait()
 
     def halo_copies(s, group):
-        part = pl.ds(group * planes, planes)
+        some = slab(group)
         return (
             pltpu.make_async_remote_copy(
-                src_ref=send_high.at[s, part], dst_ref=recv_high.at[s, part],
+                src_ref=send_high.at[s, some], dst_ref=recv_high.at[s, some],
                 send_sem=halo_send.at[s, 0, group], recv_sem=halo_recv.at[s, 0, group],
                 device_id=next_id, device_id_type=MESH),
             pltpu.make_async_remote_copy(
-                src_ref=send_low.at[s, part], dst_ref=recv_low.at[s, part],
+                src_ref=send_low.at[s, some], dst_ref=recv_low.at[s, some],
                 send_sem=halo_send.at[s, 1, group], recv_sem=halo_recv.at[s, 1, group],
                 device_id=prev_id, device_id_type=MESH),
         )
@@ -107,8 +141,11 @@
         send_low[s, k, pl.ds(b, 1), :] = value[0:1]
 
     @pl.loop(0, n)
-    def _(group):
-        @pl.loop(0, planes)
+    def _(turn):
+        group = lax.rem(part - turn + n, n)
+        in_wait(group).wait()
+
+        @pl.loop(0, planes, unroll=4)
         def _(inner):
             k = group * planes + inner
             for b in range(blocks):
@@ -131,13 +168,14 @@
         @pl.loop(0, n)
         def _(group):
             for copy in halo_copies(s, group):
-                copy.wait()
-
-        @pl.loop(0, nz)
-        def _(k):
-            for b in range(blocks):
-                source[k, b, pl.ds(0, 2), :] = recv_high[s, k, pl.ds(2 * b, 2), :]
-                source[k, b, pl.ds(rows + 2, 1), :] = recv_low[s, k, pl.ds(b, 1), :]
+                copy.wait_recv()
+
+            @pl.loop(0, planes, unroll=8)
+            def _(inner):
+                k = group * planes + inner
+                for b in range(blocks):
+                    source[k, b, pl.ds(0, 2), :] = recv_high[s, k, pl.ds(2 * b, 2), :]
+                    source[k, b, pl.ds(rows + 2, 1), :] = recv_low[s, k, pl.ds(b, 1), :]
 
         def plane(group, inner):
             k = group * planes + inner
@@ -174,30 +212,46 @@
         if s < steps - 1:
             @pl.loop(0, n)
             def _(group):
-                @pl.loop(0, planes)
+                @pl.loop(0, planes, unroll=4)
                 def _(inner):
                     plane(group, inner)
                 for copy in halo_copies(s + 1, group):
                     copy.start()
         else:
-            @pl.loop(1, n)
-            def _(i):
-                to = lax.rem(me + i, n)
-                @pl.loop(0, planes)
+            @pl.loop(0, n)
+            def _(turn):
+                to = lax.rem(me + turn + 1, n)
+
+                @pl.loop(0, planes, unroll=4)
                 def _(inner):
                     plane(to, inner)
-                out_copy(i, to, slot).start()
-            @pl.loop(0, planes)
-            def _(inner):
-                plane(me, inner)
-
-    own_out = pltpu.make_async_copy(
-        final.at[pl.ds(me * planes, planes)],
-        out_ref.at[:, pl.ds(pl.multiple_of(slot * rows, 8), rows)], local_sem.at[3])
-    own_out.start()
-    own_out.wait()
-    for i in range(1, n):
-        out_copy(i, lax.rem(me + i, n), slot_of(lax.rem(me - i + n, n), n)).wait()
+
+                @pl.when(jnp.logical_not(jnp.logical_and(is_home, to == me)))
+                def _():
+                    out_copy(to).start()
+
+    @pl.when(is_home)
+    def _():
+        out_wait(part).start()
+
+    @pl.loop(0, n)
+    def _(i):
+        @pl.when(jnp.logical_not(jnp.logical_and(is_home, i == part)))
+        def _():
+            meta_copy(i).wait_send()
+            in_copy(i).wait_send()
+
+        @pl.when(jnp.logical_not(jnp.logical_and(is_home, i == me)))
+        def _():
+            out_copy(i).wait_send()
+
+        out_wait(i).wait()
+
+    for s in range(steps):
+        @pl.loop(0, n)
+        def _(group):
+            for copy in halo_copies(s, group):
+                copy.wait_send()
 
 
 def fused(image, offsets, frac_index, fractions, n, n_xy):
@@ -215,7 +269,7 @@
     table = jnp.stack(columns, axis=1)
     tall = -(-(rows + 3) // 8) * 8
     out, _ = pl.pallas_call(
-        functools.partial(fused_kernel, n, n_xy, steps, tuple(range(1, n))),
+        functools.partial(fused_kernel, n, n_xy, steps),
         out_shape=(
             jax.ShapeDtypeStruct(image.shape, jnp.float32),
             jax.ShapeDtypeStruct((n * 8, padded), jnp.int32),
@@ -244,7 +298,7 @@
             pltpu.SemaphoreType.DMA((steps, 2, n)),
             pltpu.SemaphoreType.DMA((n,)),
             pltpu.SemaphoreType.DMA((n,)),
-            pltpu.SemaphoreType.DMA((4,)),
+            pltpu.SemaphoreType.DMA((1,)),
         ],
         compiler_params=pltpu.CompilerParams(
             collective_id=0, has_side_effects=True, vmem_limit_bytes=48 * 1024 * 1024),

time: 153 us -> 136 us (0.89)
  Pallas kernels: 146 us -> 129 us
    pallas_call x1, Pallas kernels: 146 us -> 129 us  [fused(): pl.pallas_call(functools.partial(fused_kernel, n, n_xy, steps), out_shape...]
where the time goes in v2:
time: 136 us; the launch traced here: 135 us
  Pallas kernels  129 us (95%)
  local copies, waits for them, and re-layouts  5.84 us (4%)
    pallas_call x1, Pallas kernels, fused(): pl.pallas_call(functools.partial(fused_kernel, n, n_xy, steps), out_shape...  129 us
    unnamed x8, local copies, waits for them, and re-layouts  4.74 us

profile of v2, /device:TPU:15, one launch (start us, length us, event | category | flops | bytes accessed | tf_op | source)
XLA Modules:
  0.0 135.4 jit_solution(5310784741725479753)
XLA Ops:
  0.0 0.8 fusion
  0.8 0.1 copy.25
  0.9 0.1 copy.24
  1.0 0.1 copy.23
  1.0 0.8 copy.15
  1.8 0.1 stack_reshape.6
  1.9 0.8 copy.16
  2.7 0.1 stack_reshape.7
  2.9 0.1 stack.5.table_ref
  3.0 0.0 copy-start
  3.0 1.6 %copy-done = f32[8,128,512]{2,1,0:T(8,128)S(1)} copy-done((f32[8,128,512]{2,1,0:T(8,128)S(1)}, f32[8,128,512]{2,1,0:T(8,128)}, u32[]{:S(2)}) %copy-start) | copy-done | bytes 2097176
  4.6 129.4 %shard_map.46 = (f32[8,128,512]{2,1,0:T(8,128)S(1)}, s32[64,128]{1,0:T(8,128)}) custom-call(f32[8,128,512]{2,1,0:T(8,128)S(1)} %copy-done, s32[8,128]{1,0:T(8,128)S(1)} %pad.4.meta_ref, f32[16,12]{1,0:T(8,128)S(1)} %stack.5.table_ref), custom_call_target="tpu_custom_call" | custom-call | tf_op jit(solution)/shard_map/pallas_call | solution.py:271
  134.0 1.3 copy.27
  (4 shorter events, 0.0 us)
Async XLA Ops:
  3.0 1.6 %copy-start = (f32[8,128,512]{2,1,0:T(8,128)S(1)}, f32[8,128,512]{2,1,0:T(8,128)}, u32[]{:S(2)}) copy-start(f32[8,128,512]{2,1,0:T(8,128)} %image_ref.1) | copy-start | bytes 6291460
